TPU v7x, 32 devices: a whole 2x2x4 slice. The times are simulated.
32 devices in a mesh: dp: 8 (over y, x, core), seq: 4 (over z).
Axes of the slice: x: 2, y: 2, z: 4, core: 2. Of those that a mesh axis runs over, the one named last changes fastest.
Arguments:
- student_in: bfloat16 [4096, 3584], P(('dp', 'seq')), may hold values from -6 to 6
- weight: bfloat16 [3584, 512], P(('dp', 'seq')), may hold values from -0.09375 to 0.09375
- queries: bfloat16 [4096, 512], P(('dp', 'seq')), may hold values from -8 to 8, as said below
- keys: bfloat16 [4096, 128], P(('dp', 'seq')), may hold values from -8 to 8
- values: bfloat16 [4096, 128], P(('dp', 'seq')), may hold values from -6 to 6
- lengths: int32 [8, 4], P('dp'), may hold values from 1 to 384, 512 in all within a row
- assignment: int32 [8, 4], P('dp'), may hold values from 0 to 3, each once within a row
Outputs:
- attention: bfloat16 [4096, 512], P(('dp', 'seq'))
- weight_grad: float32 [3584, 512], P(('dp', 'seq'))
Inputs may be any that keep to these rules, and one draw needn't show every extreme that they name: `queries`: entries of head 0 and of keys may reach the ends of this range. Each row holds the lengths of 4 rollouts of one sequence, summing to 512, the longest exactly 384. `assignment`: each row is a permutation of the 4 rollout blocks of one sequence.
All inputs are finite; a program needn't handle non-finite values.
Results may differ from a plain program's by a relative error of at most 0.012.
Values may be sent and summed in bfloat16 or wider, within the bound.
A program may use at most 64 MiB of HBM per device.

v0:
```python
import math
import jax
import jax.numpy as jnp
from jax import lax
from jax.sharding import PartitionSpec as P

HD = 128
HQ = 4
BLK = 128
EPSILON = 1e-06
NEGATIVE = -1e30


def locate(assign_row, doc_ends, first_slot, count):
    slot_ids = first_slot + jnp.arange(count, dtype=jnp.int32)
    block_ids = slot_ids // BLK
    block_table = jnp.arange(assign_row.shape[0], dtype=jnp.int32)
    placed = jnp.sum(
        jnp.where(block_ids[:, None] == block_table[None, :], assign_row[None, :], 0), axis=1
    )
    position = placed * BLK + slot_ids % BLK
    document = jnp.sum((position[:, None] >= doc_ends[None, :]).astype(jnp.int32), axis=1)
    return (position, document)


def absorb_block(state, key_block, value_block, query_heads, allowed):
    run_max, run_total, run_acc = state
    scores = jnp.einsum(
        "qhd,kd->hqk", query_heads, key_block, preferred_element_type=jnp.float32
    ) * HD ** (-0.5)
    masked = jnp.where(allowed[None], scores, NEGATIVE)
    new_max = jnp.maximum(run_max, jnp.max(masked, axis=-1))
    fading = jnp.exp(run_max - new_max)
    exp_terms = jnp.where(allowed[None], jnp.exp(masked - new_max[:, :, None]), 0.0)
    new_total = run_total * fading + jnp.sum(exp_terms, axis=-1)
    mixture = jnp.einsum(
        "hqk,kd->qhd",
        exp_terms.astype(jnp.bfloat16),
        value_block,
        preferred_element_type=jnp.float32,
    )
    new_acc = run_acc * fading.T[:, :, None] + mixture
    return (new_max, new_total, new_acc)


def local(student_in, weight, queries, keys, values, lengths, assignment):
    rows = queries.shape[0]
    assign_row = assignment[0]
    doc_ends = jnp.cumsum(lengths[0])
    query_pos, query_doc = locate(assign_row, doc_ends, lax.axis_index("seq") * rows, rows)
    query_heads = queries.reshape(rows, HQ, HD)
    start_state = (
        jnp.full((HQ, rows), NEGATIVE, jnp.float32),
        jnp.zeros((HQ, rows), jnp.float32),
        jnp.zeros((rows, HQ, HD), jnp.float32),
    )
    key_piece = lax.all_gather(keys, "seq", axis=0, tiled=True)
    value_piece = lax.all_gather(values, "seq", axis=0, tiled=True)
    count = key_piece.shape[0]
    step_rows = math.gcd(count, 512)
    steps_count = count // step_rows
    key_pos, key_doc = locate(assign_row, doc_ends, jnp.int32(0), count)

    def one_step(running, slabs):
        key_block, value_block, key_position, key_document = slabs
        allowed = (query_doc[:, None] == key_document[None, :]) & (
            query_pos[:, None] >= key_position[None, :]
        )
        updated = absorb_block(running, key_block, value_block, query_heads, allowed)
        return (updated, None)

    slabs = (
        key_piece.reshape(steps_count, step_rows, HD),
        value_piece.reshape(steps_count, step_rows, HD),
        key_pos.reshape(steps_count, step_rows),
        key_doc.reshape(steps_count, step_rows),
    )
    result, _ = lax.scan(one_step, start_state, slabs)
    final_max, final_total, final_acc = result
    attention = (final_acc / final_total.T[:, :, None]).reshape(rows, HQ * HD).astype(jnp.bfloat16)
    as_float = student_in.astype(jnp.float32)
    normed = (
        as_float * lax.rsqrt(jnp.mean(as_float * as_float, axis=1, keepdims=True) + EPSILON)
    ).astype(jnp.bfloat16)
    group_rows = lax.all_gather(weight, "seq", axis=0, tiled=True)
    columns = normed
    predicted = jnp.dot(
        columns,
        lax.all_gather(group_rows, "dp", axis=0, tiled=True),
        preferred_element_type=jnp.float32,
    )
    dp_count = lax.axis_size("dp")
    seq_count = lax.axis_size("seq")
    token_total = rows * dp_count * seq_count
    scaled = ((predicted - attention.astype(jnp.float32)) * token_total ** (-0.5)).astype(
        jnp.bfloat16
    )
    columns = normed
    outer_rows = lax.psum_scatter(
        lax.dot_general(
            columns, scaled, (((0,), (0,)), ((), ())), preferred_element_type=jnp.float32
        ).astype(jnp.bfloat16),
        "dp",
        scatter_dimension=0,
        tiled=True,
    )
    weight_grad = lax.psum_scatter(outer_rows, "seq", scatter_dimension=0, tiled=True).astype(
        jnp.float32
    )
    return (attention, weight_grad)


def solution(mesh):
    placed = (
        P(("dp", "seq"), None),
        P(("dp", "seq"), None),
        P(("dp", "seq"), None),
        P(("dp", "seq"), None),
        P(("dp", "seq"), None),
        P("dp", None),
        P("dp", None),
    )
    return jax.shard_map(
        local,
        mesh=mesh,
        in_specs=placed,
        out_specs=(P(("dp", "seq"), None), P(("dp", "seq"), None)),
        check_vma=False,
    )
```

profile of v0, /device:TPU:0, one launch (start us, length us, event | category | flops | bytes accessed | tf_op | source)
XLA Modules:
  0.0 149.0 jit_solution(12489444883028070864)
XLA Ops:
  7.2 0.0 copy-start
  7.2 0.0 copy-start.1
  7.2 0.0 all-gather.2.cloned.1.call-start
  7.2 18.8 %all_gather.14 = bf16[448,512]{1,0:T(8,128)(2,1)} all-gather(bf16[112,512]{1,0:T(8,128)(2,1)} %param.8), channel_id=1, replica_groups=mesh['dp'=8,'seq'=4] {'seq'}, dimensions={0}, use_global_device_ids=true | all-gather | bytes 573440 | tf_op jit(solution)/shard_map/all_gather | solution.py:85
  26.0 0.0 all-gather.2.cloned.1.call-update
  26.0 0.0 reduce-scatter.3.cloned.1.call-start
  26.1 0.9 copy.14
  26.9 0.8 reduce-window.8
  27.8 12.3 %all_gather.13 = bf16[512,128]{0,1:T(8,128)(2,1)S(1)} all-gather(bf16[128,128]{0,1:T(8,128)(2,1)S(1)} %copy.14), channel_id=1, replica_groups=mesh['dp'=8,'seq'=4] {'seq'}, dimensions={0}, use_global_device_ids=true | all-gather | bytes 163840 | tf_op jit(solution)/shard_map/all_gather | solution.py:58
  40.1 13.5 %all_gather.12 = bf16[512,128]{1,0:T(8,128)(2,1)S(1)} all-gather(bf16[128,128]{1,0:T(8,128)(2,1)} %param.10), channel_id=1, replica_groups=mesh['dp'=8,'seq'=4] {'seq'}, dimensions={0}, use_global_device_ids=true | all-gather | bytes 163840 | tf_op jit(solution)/shard_map/all_gather | solution.py:57
  53.7 0.7 select_reduce_fusion.1
  54.5 0.1 convert_reduce_fusion.1
  54.5 0.7 select_reduce_fusion
  55.3 0.1 convert_reduce_fusion
  55.4 1.4 fusion
  56.8 0.2 compare_and_fusion
  57.0 0.0 copy-done
  57.1 0.3 fusion.36
  57.4 0.2 fusion.13
  57.6 0.3 fusion.8
  58.0 2.6 %all-gather.2.cloned.1.call-done = bf16[3584,512]{1,0:T(8,128)(2,1)} async-done(((bf16[448,512]{1,0:T(8,128)(2,1)}), bf16[3584,512]{1,0:T(8,128)(2,1)}) %all-gather.2.cloned.1.call-update) | async-done | bytes 3670032 | tf_op jit(solution)/shard_map/all_gather | solution.py:89
  60.6 0.0 copy-done.1
  60.6 7.9 %convolution_convert_fusion = bf16[3584,512]{1,0:T(8,128)(2,1)} fusion(bf16[3584,512]{1,0:T(8,128)(2,1)} %all-gather.2.cloned.1.call-done, bf16[128,3584]{1,0:T(8,128)(2,1)S(1)} %copy-done.1, f32[128]{0:T(128)S(1)} %add_rsqrt_fusion, bf16[128,512]{0,1:T(8,128)(2,1)S(1)} %bitcast.40), kind=kOutput, calls=%fused_computation | convolution fusion | flops 944373760 | bytes 8389120 | tf_op jit(solution)/shard_map/dot_general | solution.py:100
  68.5 0.0 reduce-scatter.3.cloned.1.call-update
  68.6 0.0 reduce-scatter.5.cloned.1.call-start
  68.6 48.7 %reduce-scatter.3.cloned.1.call-done = bf16[448,512]{1,0:T(8,128)(2,1)} async-done(((bf16[3584,512]{1,0:T(8,128)(2,1)}), bf16[448,512]{1,0:T(8,128)(2,1)}) %reduce-scatter.3.cloned.1.call-update) | async-done | bytes 458768 | tf_op jit(solution)/shard_map/reduce_scatter | solution.py:99
  117.3 0.0 reduce-scatter.5.cloned.1.call-update
  117.3 0.8 copy.16
  118.1 22.8 %reduce-scatter.5.cloned.1.call-done = bf16[112,512]{1,0:T(8,128)(2,1)} async-done(((bf16[448,512]{1,0:T(8,128)(2,1)}), bf16[112,512]{1,0:T(8,128)(2,1)}) %reduce-scatter.5.cloned.1.call-update) | async-done | bytes 114704 | tf_op jit(solution)/shard_map/reduce_scatter | solution.py:107
  140.9 1.6 %convert_element_type.44 = f32[112,512]{1,0:T(8,128)} convert(bf16[112,512]{1,0:T(8,128)(2,1)} %reduce-scatter.5.cloned.1.call-done) | non-fusion elementwise | flops 57344 | bytes 344064 | tf_op jit(solution)/shard_map/convert_element_type | solution.py:107
  (7 shorter events, 0.1 us)
Async XLA Ops:
  7.2 49.9 %copy-start = (bf16[128,512]{1,0:T(8,128)(2,1)S(1)}, bf16[128,512]{1,0:T(8,128)(2,1)}, u32[]{:S(2)}) copy-start(bf16[128,512]{1,0:T(8,128)(2,1)} %param.9) | copy-start | bytes 393220
  7.2 53.4 %copy-start.1 = (bf16[128,3584]{1,0:T(8,128)(2,1)S(1)}, bf16[128,3584]{1,0:T(8,128)(2,1)}, u32[]{:S(2)}) copy-start(bf16[128,3584]{1,0:T(8,128)(2,1)} %param.7) | copy-start | bytes 2752516
  7.2 53.4 %all-gather.2.cloned.1.call-start = ((), (), s32[]{:S(2)}) async-start(), calls=%async_computation.2 | async-start | bytes 4128768 | tf_op jit(solution)/shard_map/all_gather | solution.py:89
  26.0 91.3 %reduce-scatter.3.cloned.1.call-start = ((), (), s32[]{:S(2)}) async-start(), calls=%async_computation.3 | async-start | bytes 4128768 | tf_op jit(solution)/shard_map/reduce_scatter | solution.py:99
  68.6 72.3 %reduce-scatter.5.cloned.1.call-start = ((), (), s32[]{:S(2)}) async-start(), calls=%async_computation.4 | async-start | bytes 573440 | tf_op jit(solution)/shard_map/reduce_scatter | solution.py:107
Sparse Core Ops, SparseCore 0:
  26.1 34.3 all-gather.1
  68.7 48.5 reduce-scatter.2
  119.6 21.2 reduce-scatter.4
where the time goes:
time: 149 us
  waiting for transfers between devices  74.2 us (50%)
  blocking collectives  44.7 us (30%)
  between operations  13.8 us (9%)
  matrix products  8.59 us (6%)
  other arithmetic  6.01 us (4%)
  local copies, waits for them, and re-layouts  1.65 us (1%)
    reduce_scatter x1, waiting for transfers between devices, local(): lax.psum_scatter(lax.dot_general(columns, scaled, (((0,), (0,)), ((), ())...  48.7 us
    reduce_scatter x1, waiting for transfers between devices, local(): lax.psum_scatter(outer_rows, 'seq', scatter_dimension=0, tiled=True)  22.8 us
    all_gather x1, blocking collectives, local(): group_rows = lax.all_gather(weight, 'seq', axis=0, tiled=True)  18.8 us
    all_gather x1, blocking collectives, local(): key_piece = lax.all_gather(keys, 'seq', axis=0, tiled=True)  13.5 us
    all_gather x1, blocking collectives, local(): value_piece = lax.all_gather(values, 'seq', axis=0, tiled=True)  12.3 us
    dot_general x1, matrix products, local(): lax.dot_general(columns, scaled, (((0,), (0,)), ((), ())), preferred_elem...  7.94 us
  transfers between devices with their start and end apart: 3, of which 3 were waited for; matrix products, arithmetic and copies ran while one was open for 4% of the time, Pallas kernels for 0%

commit v1 on v0

--- a/solution.py
+++ b/solution.py
@@ -55,7 +55,12 @@
         jnp.zeros((rows, HQ, HD), jnp.float32),
     )
     key_piece = lax.all_gather(keys, "seq", axis=0, tiled=True)
-    value_piece = lax.all_gather(values, "seq", axis=0, tiled=True)
+    ring = [values]
+    for hop in range(3):
+        ring.append(lax.ppermute(ring[-1], "seq", [(dev, (dev + 1) % 4) for dev in range(4)]))
+    value_piece = jnp.roll(
+        jnp.concatenate(ring[::-1], axis=0), (lax.axis_index("seq") + 1) * ring[0].shape[0], axis=0
+    )
     count = key_piece.shape[0]
     step_rows = math.gcd(count, 512)
     steps_count = count // step_rows

time: 149 us -> 149 us (level)
  blocking collectives: 44.7 us -> 32.8 us
  waiting for transfers between devices: 74.2 us -> 85.3 us
  starting transfers between devices: 0.12 us -> 1.92 us
    all_gather x1 -> x0, blocking collectives: 12.3 us -> none  [local(): value_piece = lax.all_gather(values, 'seq', axis=0, tiled=True)]
    ppermute x0 -> x3, waiting for transfers between devices: none -> 9.88 us  [local(): lax.ppermute(ring[-1], 'seq', [(dev, (dev + 1) % 4) for dev in range(4)])]
    ppermute x0 -> x3, starting transfers between devices: none -> 1.8 us  [local(): lax.ppermute(ring[-1], 'seq', [(dev, (dev + 1) % 4) for dev in range(4)])]
  transfers between devices with their start and end apart: 3 -> 6, of which waited for: 3 -> 5; matrix products, arithmetic and copies ran while one was open for 4% -> 4% of each run, Pallas kernels for 0% -> 0%
where the time goes in v1:
time: 149 us
  waiting for transfers between devices  85.3 us (57%)
  blocking collectives  32.8 us (22%)
  between operations  13.9 us (9%)
  matrix products  8.58 us (6%)
  other arithmetic  4.83 us (3%)
  starting transfers between devices  1.92 us (1%)
  local copies, waits for them, and re-layouts  1.75 us (1%)
    reduce_scatter x1, waiting for transfers between devices, local(): lax.psum_scatter(lax.dot_general(columns, scaled, (((0,), (0,)), ((), ())...  48.7 us
    reduce_scatter x1, waiting for transfers between devices, local(): lax.psum_scatter(outer_rows, 'seq', scatter_dimension=0, tiled=True)  22.8 us
    all_gather x1, blocking collectives, local(): group_rows = lax.all_gather(weight, 'seq', axis=0, tiled=True)  18.8 us
    all_gather x1, blocking collectives, local(): key_piece = lax.all_gather(keys, 'seq', axis=0, tiled=True)  14 us
    ppermute x3, waiting for transfers between devices, local(): lax.ppermute(ring[-1], 'seq', [(dev, (dev + 1) % 4) for dev in range(4)])  9.88 us
    dot_general x1, matrix products, local(): lax.dot_general(columns, scaled, (((0,), (0,)), ((), ())), preferred_elem...  7.94 us
    all_gather x1, waiting for transfers between devices, local(): lax.all_gather(group_rows, 'dp', axis=0, tiled=True)  3.91 us
  transfers between devices with their start and end apart: 6, of which 5 were waited for; matrix products, arithmetic and copies ran while one was open for 4% of the time, Pallas kernels for 0%

profile of v1, /device:TPU:0, one launch (start us, length us, event | category | flops | bytes accessed | tf_op | source)
XLA Modules:
  0.0 149.0 jit_solution(4657982836793132429)
XLA Ops:
  7.2 0.0 copy-start
  7.2 0.0 copy-start.1
  7.2 0.0 all-gather.2.cloned.1.call-start
  7.2 18.8 %all_gather.10 = bf16[448,512]{1,0:T(8,128)(2,1)} all-gather(bf16[112,512]{1,0:T(8,128)(2,1)} %param.8), channel_id=1, replica_groups=mesh['dp'=8,'seq'=4] {'seq'}, dimensions={0}, use_global_device_ids=true | all-gather | bytes 573440 | tf_op jit(solution)/shard_map/all_gather | solution.py:90
  26.0 0.0 all-gather.2.cloned.1.call-update
  26.0 0.0 reduce-scatter.3.cloned.1.call-start
  26.1 0.9 copy.16
  26.9 0.5 collective-permute-start
  27.4 0.8 reduce-window.8
  28.2 14.0 %all_gather.9 = bf16[512,128]{1,0:T(8,128)(2,1)S(1)} all-gather(bf16[128,128]{1,0:T(8,128)(2,1)} %param.10), channel_id=1, replica_groups=mesh['dp'=8,'seq'=4] {'seq'}, dimensions={0}, use_global_device_ids=true | all-gather | bytes 163840 | tf_op jit(solution)/shard_map/all_gather | solution.py:57
  42.3 0.7 select_reduce_fusion.1
  43.0 0.1 convert_reduce_fusion.1
  43.1 0.7 select_reduce_fusion
  43.9 0.1 convert_reduce_fusion
  43.9 0.2 compare_and_fusion
  44.2 0.0 copy-done
  44.2 0.3 fusion.38
  44.5 0.2 fusion.13
  44.7 0.0 collective-permute-done
  44.7 1.3 collective-permute-start.1
  46.1 0.0 copy-done.1
  46.1 0.3 fusion
  46.3 4.2 %collective-permute-done.1 = bf16[128,128]{0,1:T(8,128)(2,1)S(1)} collective-permute-done((bf16[128,128]{0,1:T(8,128)(2,1)S(1)}, bf16[128,128]{0,1:T(8,128)(2,1)S(1)}, u32[]{:S(2)}, u32[]{:S(2)}) %collective-permute-start.1) | collective-permute-done | bytes 32800 | tf_op jit(solution)/shard_map/ppermute | solution.py:60
  50.5 0.0 collective-permute-start.2
  50.5 5.7 %collective-permute-done.2 = bf16[128,128]{0,1:T(8,128)(2,1)S(1)} collective-permute-done((bf16[128,128]{0,1:T(8,128)(2,1)S(1)}, bf16[128,128]{0,1:T(8,128)(2,1)S(1)}, u32[]{:S(2)}, u32[]{:S(2)}) %collective-permute-start.2) | collective-permute-done | bytes 32800 | tf_op jit(solution)/shard_map/ppermute | solution.py:60
  56.3 0.3 fusion.8
  56.7 3.9 %all-gather.2.cloned.1.call-done = bf16[3584,512]{1,0:T(8,128)(2,1)} async-done(((bf16[448,512]{1,0:T(8,128)(2,1)}), bf16[3584,512]{1,0:T(8,128)(2,1)}) %all-gather.2.cloned.1.call-update) | async-done | bytes 3670032 | tf_op jit(solution)/shard_map/all_gather | solution.py:94
  60.6 7.9 %convolution_convert_fusion = bf16[3584,512]{1,0:T(8,128)(2,1)} fusion(bf16[3584,512]{1,0:T(8,128)(2,1)} %all-gather.2.cloned.1.call-done, bf16[128,3584]{1,0:T(8,128)(2,1)S(1)} %copy-done.1, f32[128]{0:T(128)S(1)} %add_rsqrt_fusion, bf16[128,512]{0,1:T(8,128)(2,1)S(1)} %bitcast.40), kind=kOutput, calls=%fused_computation | convolution fusion | flops 944373760 | bytes 8389120 | tf_op jit(solution)/shard_map/dot_general | solution.py:105
  68.5 0.0 reduce-scatter.3.cloned.1.call-update
  68.6 0.0 reduce-scatter.5.cloned.1.call-start
  68.6 48.7 %reduce-scatter.3.cloned.1.call-done = bf16[448,512]{1,0:T(8,128)(2,1)} async-done(((bf16[3584,512]{1,0:T(8,128)(2,1)}), bf16[448,512]{1,0:T(8,128)(2,1)}) %reduce-scatter.3.cloned.1.call-update) | async-done | bytes 458768 | tf_op jit(solution)/shard_map/reduce_scatter | solution.py:104
  117.3 0.0 reduce-scatter.5.cloned.1.call-update
  117.3 0.8 copy.20
  118.1 22.8 %reduce-scatter.5.cloned.1.call-done = bf16[112,512]{1,0:T(8,128)(2,1)} async-done(((bf16[448,512]{1,0:T(8,128)(2,1)}), bf16[112,512]{1,0:T(8,128)(2,1)}) %reduce-scatter.5.cloned.1.call-update) | async-done | bytes 114704 | tf_op jit(solution)/shard_map/reduce_scatter | solution.py:112
  140.9 1.6 %convert_element_type.44 = f32[112,512]{1,0:T(8,128)} convert(bf16[112,512]{1,0:T(8,128)(2,1)} %reduce-scatter.5.cloned.1.call-done) | non-fusion elementwise | flops 57344 | bytes 344064 | tf_op jit(solution)/shard_map/convert_element_type | solution.py:112
  (15 shorter events, 0.2 us)
Async XLA Ops:
  7.2 37.0 %copy-start = (bf16[128,512]{1,0:T(8,128)(2,1)S(1)}, bf16[128,512]{1,0:T(8,128)(2,1)}, u32[]{:S(2)}) copy-start(bf16[128,512]{1,0:T(8,128)(2,1)} %param.9) | copy-start | bytes 393220
  7.2 38.9 %copy-start.1 = (bf16[128,3584]{1,0:T(8,128)(2,1)S(1)}, bf16[128,3584]{1,0:T(8,128)(2,1)}, u32[]{:S(2)}) copy-start(bf16[128,3584]{1,0:T(8,128)(2,1)} %param.7) | copy-start | bytes 2752516
  7.2 53.4 %all-gather.2.cloned.1.call-start = ((), (), s32[]{:S(2)}) async-start(), calls=%async_computation.2 | async-start | bytes 4128768 | tf_op jit(solution)/shard_map/all_gather | solution.py:94
  26.0 91.2 %reduce-scatter.3.cloned.1.call-start = ((), (), s32[]{:S(2)}) async-start(), calls=%async_computation.3 | async-start | bytes 4128768 | tf_op jit(solution)/shard_map/reduce_scatter | solution.py:104
  26.9 17.8 %collective-permute-start = (bf16[128,128]{0,1:T(8,128)(2,1)S(1)}, bf16[128,128]{0,1:T(8,128)(2,1)S(1)}, u32[]{:S(2)}, u32[]{:S(2)}) collective-permute-start(bf16[128,128]{0,1:T(8,128)(2,1)S(1)} %copy.16), channel_id=1, source_target_pairs={{0,1},{1,2},{2,3},{3,0},{4,5},{5,6},{6,7},{7,4},{8,9},{9,10},{10,1... | collective-permute-start | bytes 98312 | tf_op jit(solution)/shard_map/ppermute | solution.py:60
  44.7 5.8 %collective-permute-start.1 = (bf16[128,128]{0,1:T(8,128)(2,1)S(1)}, bf16[128,128]{0,1:T(8,128)(2,1)S(1)}, u32[]{:S(2)}, u32[]{:S(2)}) collective-permute-start(bf16[128,128]{0,1:T(8,128)(2,1)S(1)} %collective-permute-done), channel_id=1, source_target_pairs={{0,1},{1,2},{2,3},{3,0},{4,5},{5,6},{6,7},{7,4},{8,9},{9,10},{10,1... | collective-permute-start | bytes 98312 | tf_op jit(solution)/shard_map/ppermute | solution.py:60
  50.5 5.7 %collective-permute-start.2 = (bf16[128,128]{0,1:T(8,128)(2,1)S(1)}, bf16[128,128]{0,1:T(8,128)(2,1)S(1)}, u32[]{:S(2)}, u32[]{:S(2)}) collective-permute-start(bf16[128,128]{0,1:T(8,128)(2,1)S(1)} %collective-permute-done.1), channel_id=1, source_target_pairs={{0,1},{1,2},{2,3},{3,0},{4,5},{5,6},{6,7},{7,4},{8,9},{9,10},{10,1... | collective-permute-start | bytes 98312 | tf_op jit(solution)/shard_map/ppermute | solution.py:60
  68.6 72.3 %reduce-scatter.5.cloned.1.call-start = ((), (), s32[]{:S(2)}) async-start(), calls=%async_computation.4 | async-start | bytes 573440 | tf_op jit(solution)/shard_map/reduce_scatter | solution.py:112
Sparse Core Ops, SparseCore 0:
  26.1 34.3 all-gather.1
  68.7 48.5 reduce-scatter.2
  119.6 21.2 reduce-scatter.4
